TPU v7x, 32 devices: a whole 2x2x4 slice. The times are simulated.
32 devices in a mesh: scene: 2 (over x), az: 16 (over z, y, core).
Axes of the slice: x: 2, y: 2, z: 4, core: 2. Of those that a mesh axis runs over, the one named last changes fastest.
Arguments:
- secondary: bfloat16 [2, 512, 12288], P(None, ('scene', 'az')), parts along dimension 1, may hold values from -6 to 6
- line_valid: int32 [512], P(('scene', 'az')), parts along dimension 0, may hold values 0 or 1
- first_valid: int32 [512], P(('scene', 'az')), parts along dimension 0, may hold values from 0 to 3071
- last_valid: int32 [512], P(('scene', 'az')), parts along dimension 0, may hold values from 9216 to 12288
- az_coef: float32 [3, 512], P(None, ('scene', 'az')), parts along dimension 1, may hold values from -0.33 to 0.33
- az_base: int32 [512], P(('scene', 'az')), parts along dimension 0, may hold values from -3 to 3
- rg_base: int32 [512], P(('scene', 'az')), parts along dimension 0, may hold values from -8 to 8
- rg_coef: float32 [8], P('scene'), parts along dimension 0, may hold values from -3 to 3
- block_dest: int32 [512], P(('scene', 'az')), parts along dimension 0, may hold values from 0 to 255, as said below
Outputs:
- coreg: bfloat16 [2, 512, 12288], P(None, ('scene', 'az')), parts along dimension 1
- mean_power: float32 [2], P('scene'), parts along dimension 0
- valid_share: float32 [2], P('scene'), parts along dimension 0
There are 2 independent parts, one for each index of `scene`. A program takes and returns all parts, laid end to end along the dimension named above; each array names one. Nothing has to cross between parts.
Inputs may be any that keep to these rules, and one draw needn't show every extreme that they name: `block_dest`: A permutation of 0 to 255. The 16 line blocks of each device of az take exactly one place on every device of az, itself included (place // 16 runs over all devices).
All inputs are finite; a program needn't handle non-finite values. No bound on the sum of `line_valid` on one device may be relied on, other than what follows from the above.
Results may differ from a plain program's by a relative error of at most 0.0066.
Values may be sent and summed in bfloat16 or wider, within the bound.
A program may use at most 128 MiB of HBM per device.

v0:
```python
import functools

import jax
import jax.numpy as jnp
from jax import lax
from jax.experimental import pallas as pl
from jax.experimental.pallas import tpu as pltpu
from jax.sharding import PartitionSpec as P

HALO = 8
TAPS = 11
NOTE = 8
STEP = 512
PI = 3.141592653589793
HALF = 0.7071067811865476
COS8 = (1.0, HALF, 0.0, -HALF, -1.0, -HALF, 0.0, HALF)


def range_weights(coef, start, weight, cols):
    for g in range(cols // 1024):
        centre = (g * 1024 + 512) / cols
        oc = coef[0] + coef[1] * centre + coef[2] * (centre * centre) + coef[3] * (centre**3)
        n0 = (oc - 5.0 + 64.0).astype(jnp.int32) - 63
        start[g] = n0
        sub = lax.broadcasted_iota(jnp.int32, (8, 128), 0)
        lane = lax.broadcasted_iota(jnp.int32, (8, 128), 1)
        col = g * 1024 + sub * 128 + lane
        v = (col.astype(jnp.float32) + 0.5) / cols
        off = coef[0] + coef[1] * v + coef[2] * v * v + coef[3] * v * v * v
        whole = jnp.round(off)
        part = off - whole
        odd = (whole.astype(jnp.int32) + n0) & 1
        sine = jnp.sin(PI * part) * (-1.0 / PI) * (1 - 2 * odd).astype(jnp.float32)
        base = (n0.astype(jnp.float32) - off) * (PI / 4.0)
        c0, s0 = jnp.cos(base), jnp.sin(base)
        for k in range(TAPS):
            n = n0 + k
            d = n.astype(jnp.float32) - off
            ck, sk = COS8[k % 8], COS8[(k - 2) % 8]
            taper = 0.5 + 0.5 * (c0 * ck - s0 * sk)
            top = sine if k % 2 == 0 else -sine
            near = d == 0.0
            val = jnp.where(near, 1.0, top / jnp.where(near, 1.0, d)) * taper
            keep = (jnp.abs(d) < 4.0) & (col + n >= 0) & (col + n < cols)
            val = jnp.where(keep, val, 0.0)
            weight[g, k] = val.astype(jnp.bfloat16).astype(jnp.float32)


def column(values):
    row = lax.broadcasted_iota(jnp.int32, (len(values), 128), 0)
    made = jnp.zeros((len(values), 128), jnp.asarray(values[0]).dtype)
    for r, value in enumerate(values):
        made = jnp.where(row == r, value, made)
    return made


def azimuth_band(fraction, base, line, blocks):
    held = lax.broadcasted_iota(jnp.int32, (blocks, 128), 1)
    row = jnp.where(held < blocks, held, held - blocks - HALO)
    row = jnp.where(held < blocks + HALO, row, held - HALO)
    gap = row - line - base
    d = gap.astype(jnp.float32) - fraction
    near = d == 0.0
    safe = jnp.where(near, 1.0, d)
    whole = jnp.round(safe)
    sine = jnp.sin(PI * (safe - whole)) * (1 - 2 * (whole.astype(jnp.int32) & 1)).astype(jnp.float32)
    value = jnp.where(near, 1.0, sine / (PI * safe)) * (0.5 + 0.5 * jnp.cos(PI * d / 4.0))
    keep = (jnp.abs(d) < 4.0) & (jnp.abs(gap) <= 4) & (held < blocks + 2 * HALO)
    return jnp.where(keep, value, 0.0).astype(jnp.bfloat16)


def send_order(me, count, i):
    half = count // 2
    mine = me // half
    own = i // half
    side = mine * own + (1 - mine) * (1 - own)
    return side * half + lax.rem(me - mine * half + own + i - own * half, half)


def swath_kernel(
    cuts, coef, shift, dest, valid, first, last, az_coef, az_base, image,
    got, notes,
    held, edge, dense, weight, sent, memo, start, order,
    ready, own_sem, halo_send, halo_recv, edge_send, edge_recv, send_sem, recv_sem, note_send, note_recv,
):
    blocks, cols = image.shape[1], image.shape[2]
    tiles = cols // 128
    span = dense.shape[0] // (2 * blocks)
    count = lax.axis_size("az")
    me = lax.axis_index("az")
    after, before = lax.rem(me + 1, count), lax.rem(me + count - 1, count)
    own = pltpu.make_async_copy(image, held.at[:, pl.ds(0, blocks)], own_sem)
    own.start()

    barrier = pltpu.get_barrier_semaphore()

    for peer in (after, before):
        pl.semaphore_signal(barrier, inc=1, device_id={"az": peer})
    low_edge = [jnp.where(valid[r] > 0, first[r], cols) for r in range(blocks)]
    high_edge = [jnp.where(valid[r] > 0, last[r], 0) for r in range(blocks)]
    edge[0, pl.ds(0, blocks), :] = column(low_edge).astype(jnp.float32)
    edge[1, pl.ds(0, blocks), :] = column(high_edge).astype(jnp.float32)
    pl.semaphore_wait(barrier, 2)

    steps = cols // STEP
    chunks = len(cuts) - 1
    per = steps // (tiles // 16)
    bounds = [0] + [cut * per + 1 for cut in cuts[1:-1]] + [steps]
    ways = ((after, blocks - HALO, blocks), (before, 0, blocks + HALO))
    for w, (peer, source, slot) in enumerate(ways):
        pltpu.make_async_remote_copy(
            src_ref=edge.at[:, pl.ds(source, HALO), :],
            dst_ref=edge.at[:, pl.ds(slot, HALO), :],
            send_sem=edge_send.at[w],
            recv_sem=edge_recv.at[w],
            device_id={"az": peer},
        ).start()
    halo = []
    for c in range(chunks):
        at = pl.ds(bounds[c] * STEP, (bounds[c + 1] - bounds[c]) * STEP)
        for w, (peer, source, slot) in enumerate(ways):
            copy = pltpu.make_async_remote_copy(
                src_ref=image.at[:, pl.ds(source, HALO), at],
                dst_ref=held.at[:, pl.ds(slot, HALO), at],
                send_sem=halo_send.at[c, w],
                recv_sem=halo_recv.at[c, w],
                device_id={"az": peer},
            )
            copy.start()
            halo.append(copy)

    def meet(r):
        for peer in (lax.rem(me + (1 << r), count), lax.rem(me + count - (1 << r), count)):
            pl.semaphore_signal(ready.at[r], inc=1, device_id={"az": peer})

    meetings = ready.shape[0]
    meet(0)
    lines = []
    for i in range(blocks):
        target = send_order(me, count, i)
        line = jnp.int32(0)
        for j in range(blocks):
            line = jnp.where(dest[j] // blocks == target, j, line)
        order[i] = line
        lines.append(line)
    c0 = column([az_coef[0, j] for j in lines])
    c1 = column([az_coef[1, j] for j in lines])
    c2 = column([az_coef[2, j] for j in lines])
    q = 0.5
    fraction = c0 + c1 * q + c2 * q * q
    band = azimuth_band(fraction, column([az_base[j] for j in lines]), column(lines), blocks)
    band = band[:, : blocks + 2 * HALO]
    pl.semaphore_wait(ready.at[0], 2)
    if meetings > 1:
        meet(1)
    range_weights(coef, start, weight, cols)
    for r in range(1, meetings):
        pl.semaphore_wait(ready.at[r], 2)
        if r + 1 < meetings:
            meet(r + 1)

    own.wait()
    for w, (peer, source, slot) in enumerate(ways):
        pltpu.make_async_remote_copy(
            src_ref=edge.at[:, pl.ds(source, HALO), :],
            dst_ref=edge.at[:, pl.ds(slot, HALO), :],
            send_sem=edge_send.at[w],
            recv_sem=edge_recv.at[w],
            device_id={"az": peer},
        ).wait()
    low = edge[0]
    high = edge[1]
    row = lax.broadcasted_iota(jnp.int32, high.shape, 0)
    outside = ((me == 0) & (row >= blocks) & (row < blocks + HALO)) | (
        (me == count - 1) & (row >= blocks + HALO)
    )
    high = jnp.where(outside, 0.0, high)
    lane_held = lax.broadcasted_iota(jnp.int32, high.shape, 1).astype(jnp.float32)
    lane_row = lax.broadcasted_iota(jnp.int32, (blocks, 128), 1)
    lane = lax.broadcasted_iota(jnp.int32, (8, 128), 1)

    def azimuth(s, tails):
        at = pl.ds(pl.multiple_of(s * STEP, STEP), STEP)
        keeps = []
        for u in range(STEP // 128):
            col = lane_held + (s * STEP + u * 128).astype(jnp.float32)
            keeps.append((col >= low) & (col < high))
        new_tails = []
        for p in range(2):
            rows = held[p, :, at].astype(jnp.float32)
            rows = jnp.concatenate(
                [
                    jnp.where(keep, rows[:, u * 128 : u * 128 + 128], 0.0)
                    for u, keep in enumerate(keeps)
                ],
                axis=1,
            ).astype(jnp.bfloat16)
            out = jnp.dot(band, rows, preferred_element_type=jnp.float32)
            out = out.astype(jnp.bfloat16).astype(jnp.float32)
            tail = tails[p]
            for u in range(STEP // 128):
                turned = pltpu.roll(out[:, u * 128 : u * 128 + 128], 64, 1)
                place = p * blocks * span + s * (STEP // 128) + u
                dense[pl.ds(place, blocks, stride=span), :] = jnp.where(lane_row < 64, tail, turned)
                tail = turned
            new_tails.append(tail)
        return tuple(new_tails)

    def filtered(i, big, power):
        for p in range(2):
            halves = []
            for h in range(2):
                g = big * 2 + h
                b = shift[order[i]] + start[g] + 64
                at = pl.multiple_of((p * blocks + i) * span + g * 8, 8)
                x0 = dense[pl.ds(at, 8), :]
                x1 = dense[pl.ds(at + 1, 8), :]
                acc = None
                for k in range(TAPS):
                    moved = pltpu.roll(jnp.where(lane < b + k, x1, x0), 128 - b - k, 1)
                    term = weight[g, k] * moved
                    acc = term if acc is None else acc + term
                halves.append(acc)
            done = jnp.concatenate(halves, axis=0).astype(jnp.bfloat16)
            sent[i, p, pl.ds(pl.multiple_of(big * 16, 16), 16), :] = done
            wide = done.astype(jnp.float32)
            power = power + wide * wide
        return power

    tails = (jnp.zeros((blocks, 128), jnp.float32),) * 2
    power = jnp.zeros((16, 128), jnp.float32)
    for c in range(chunks):
        for copy in halo[2 * c : 2 * c + 2]:
            copy.wait()
        tails = lax.fori_loop(bounds[c], bounds[c + 1], azimuth, tails)
        if c == chunks - 1:
            for p in range(2):
                ends = jnp.where(lane_row < 64, tails[p], 0.0)
                dense[pl.ds(p * blocks * span + tiles, blocks, stride=span), :] = ends
        lo, hi = cuts[c], cuts[c + 1]
        at = pl.ds(lo * 16, (hi - lo) * 16)

        def line(i, power):
            power = lax.fori_loop(lo, hi, functools.partial(filtered, i), power, unroll=True)

            @pl.when(i < count - 1)
            def _():
                pltpu.make_async_remote_copy(
                    src_ref=sent.at[i, :, at, :],
                    dst_ref=got.at[me, :, at, :],
                    send_sem=send_sem.at[c, i],
                    recv_sem=recv_sem.at[c, me],
                    device_id={"az": send_order(me, count, i)},
                ).start()

            return power

        power = lax.fori_loop(0, blocks, line, power)

    own_power = jnp.broadcast_to(jnp.sum(power, keepdims=True), (NOTE, 128))
    have = jnp.int32(0)
    for j in range(blocks):
        have = have + jnp.maximum(
            jnp.minimum(high_edge[j], cols) - jnp.maximum(low_edge[j], 0), 0
        )
    own_count = jnp.full((NOTE, 128), have, jnp.int32).astype(jnp.float32)
    row = lax.broadcasted_iota(jnp.int32, (NOTE, 128), 0)
    stats = jnp.where(row == 1, own_power, own_count)
    for i in range(blocks):
        place = jnp.full((NOTE, 128), dest[lines[i]] % blocks, jnp.int32).astype(jnp.float32)
        memo[i] = jnp.where(row == 0, place, stats)

    def tell(i, carry):
        pltpu.make_async_remote_copy(
            src_ref=memo.at[i],
            dst_ref=notes.at[me],
            send_sem=note_send.at[i],
            recv_sem=note_recv.at[me],
            device_id={"az": send_order(me, count, i)},
        ).start()
        return carry

    lax.fori_loop(0, count - 1, tell, 0)
    notes[me] = memo[blocks - 1]
    got[me] = sent[blocks - 1]

    def take(i, carry):
        peer = send_order(me, count, i)
        for c in range(chunks):
            lo, hi = cuts[c], cuts[c + 1]
            at = pl.ds(lo * 16, (hi - lo) * 16)
            done = pltpu.make_async_remote_copy(
                src_ref=sent.at[i, :, at, :],
                dst_ref=got.at[peer, :, at, :],
                send_sem=send_sem.at[c, i],
                recv_sem=recv_sem.at[c, peer],
                device_id={"az": peer},
            )
            done.wait_send()
            done.wait_recv()
        told = pltpu.make_async_remote_copy(
            src_ref=memo.at[i],
            dst_ref=notes.at[peer],
            send_sem=note_send.at[i],
            recv_sem=note_recv.at[peer],
            device_id={"az": peer},
        )
        told.wait_send()
        told.wait_recv()
        return carry

    lax.fori_loop(0, count - 1, take, 0)


def finish_kernel(total, got, notes, out, mean, share, wide):
    blocks, cols = out.shape[1], out.shape[2]
    tiles = cols // 128
    told = [notes[s] for s in range(blocks)]
    both = functools.reduce(lambda a, b: a + b, told)
    power, count = both[1:2], both[2:3]
    mean_power = power / jnp.maximum(count, 1.0)
    gain = lax.rsqrt(mean_power + 0.5)
    mean[0] = mean_power[0, 0]
    share[0] = (count / float(total))[0, 0]
    for s in range(blocks):
        place = told[s][0, 0].astype(jnp.int32)
        for p in range(2):
            x = got[s, p].astype(jnp.float32) * gain
            wide[pl.ds(pl.multiple_of((p * blocks + place) * tiles, 8), tiles), :] = x
    for t in range(tiles):
        for p in range(2):
            x = wide[pl.ds(p * blocks * tiles + t, blocks, stride=tiles), :]
            out[p, :, t * 128 : t * 128 + 128] = x.astype(jnp.bfloat16)


def shards(
    secondary, line_valid, first_valid, last_valid, az_coef, az_base, rg_base, rg_coef, block_dest
):
    cols = secondary.shape[2]
    blocks = block_dest.shape[0]
    tiles = cols // 128
    count = lax.axis_size("az")
    bigs = tiles // 16
    cuts = [0] + sorted({bigs * cut // 6 for cut in CUTS} - {0, bigs}) + [bigs]
    chunks = len(cuts) - 1
    parts = max(c for c in range(1, PARTS + 1) if bigs % c == 0)
    smem = pl.BlockSpec(memory_space=pltpu.SMEM)
    vmem = pl.BlockSpec(memory_space=pltpu.VMEM)
    held = blocks + 2 * HALO
    dma = pltpu.SemaphoreType.DMA
    got, notes = pl.pallas_call(
        functools.partial(swath_kernel, cuts),
        out_shape=(
            jax.ShapeDtypeStruct((blocks, 2, tiles, 128), jnp.bfloat16),
            jax.ShapeDtypeStruct((blocks, NOTE, 128), jnp.float32),
        ),
        in_specs=[smem] * 8 + [pl.BlockSpec(memory_space=pl.ANY)],
        out_specs=(vmem, vmem),
        scratch_shapes=[
            pltpu.VMEM((2, held, cols), jnp.bfloat16),
            pltpu.VMEM((2, held, 128), jnp.float32),
            pltpu.VMEM((2 * blocks * (tiles + 8), 128), jnp.float32),
            pltpu.VMEM((tiles // 8, TAPS, 8, 128), jnp.float32),
            pltpu.VMEM((blocks, 2, tiles, 128), jnp.bfloat16),
            pltpu.VMEM((blocks, NOTE, 128), jnp.float32),
            pltpu.SMEM((tiles // 8,), jnp.int32),
            pltpu.SMEM((blocks,), jnp.int32),
            pltpu.SemaphoreType.REGULAR((max(1, (count // 2 - 1).bit_length()),)),
            dma(()),
            dma((chunks, 2)),
            dma((chunks, 2)),
            dma((2,)),
            dma((2,)),
            dma((chunks, blocks)),
            dma((chunks, blocks)),
            dma((blocks,)),
            dma((blocks,)),
        ],
        compiler_params=pltpu.CompilerParams(collective_id=0, has_side_effects=True),
        name="swath",
    )(
        rg_coef, rg_base, block_dest, line_valid, first_valid, last_valid, az_coef, az_base,
        secondary,
    )
    return pl.pallas_call(
        functools.partial(finish_kernel, cols * blocks * count),
        out_shape=(
            jax.ShapeDtypeStruct((2, blocks, cols), jnp.bfloat16),
            jax.ShapeDtypeStruct((1,), jnp.float32),
            jax.ShapeDtypeStruct((1,), jnp.float32),
        ),
        grid=(parts,),
        in_specs=[pl.BlockSpec((blocks, 2, tiles // parts, 128), lambda c: (0, 0, c, 0)), vmem],
        out_specs=(pl.BlockSpec((2, blocks, cols // parts), lambda c: (0, 0, c)), smem, smem),
        scratch_shapes=[pltpu.VMEM((2 * blocks * (tiles // parts), 128), jnp.float32)],
        name="finish",
    )(got, notes)


CUTS = (2,)
PARTS = 2


def solution(mesh):
    rows = P(("scene", "az"))
    placed = (
        P(None, ("scene", "az"), None),
        rows,
        rows,
        rows,
        P(None, ("scene", "az")),
        rows,
        rows,
        P("scene"),
        rows,
    )
    return jax.shard_map(
        shards,
        mesh=mesh,
        in_specs=placed,
        out_specs=(P(None, ("scene", "az"), None), P("scene"), P("scene")),
        check_vma=False,
    )
```

profile of v0, /device:TPU:0, one launch (start us, length us, event | category | flops | bytes accessed | tf_op | source)
XLA Modules:
  0.0 39.4 jit_solution(5014366095657084133)
XLA Ops:
  0.6 36.2 %swath.1 = (bf16[16,2,96,128]{3,2,1,0:T(8,128)(2,1)}, f32[16,8,128]{2,1,0:T(8,128)}) custom-call(f32[4]{0:T(128)} %coef.1, s32[16]{0:T(128)} %shift.1, s32[16]{0:T(128)} %dest.1, s32[16]{0:T(128)} %valid.1, s32[16]{0:T(128)} %first.1, s32[16]{0:T(128)} %last.1, f32[3,16]{1,0:T(4,128)} %az_coef.1, s32[16]{0:T(128)} %az_base.1, bf16[2,16,12288]{2,1,0:T(8,128)(2,1)} %image.1), custom_call_target="tpu_custom_call" | custom-call | tf_op jit(solution)/shard_map/swath/pallas_call | solution.py:351
  36.8 2.6 %finish.1 = (bf16[2,16,12288]{2,1,0:T(8,128)(2,1)}, f32[1]{0:T(128)}, f32[1]{0:T(128)}) custom-call(bf16[16,2,96,128]{3,2,1,0:T(8,128)(2,1)} %get-tuple-element.5.got, f32[16,8,128]{2,1,0:T(8,128)} %get-tuple-element.6.notes), custom_call_target="tpu_custom_call" | custom-call | tf_op jit(solution)/shard_map/finish/pallas_call | solution.py:385
where the time goes:
time: 39.6 us; the launch traced here: 39.4 us
  Pallas kernels  38.8 us (98%)
  between operations  0.64 us (2%)
    pallas_call x1, Pallas kernels, shards(): pl.pallas_call(functools.partial(swath_kernel, cuts), out_shape=(jax.Shap...  36.2 us
    pallas_call x1, Pallas kernels, shards(): pl.pallas_call(functools.partial(finish_kernel, cols * blocks * count), o...  2.55 us

commit v1 on v0

--- a/solution.py
+++ b/solution.py
@@ -10,7 +10,6 @@
 HALO = 8
 TAPS = 11
 NOTE = 8
-STEP = 512
 PI = 3.141592653589793
 HALF = 0.7071067811865476
 COS8 = (1.0, HALF, 0.0, -HALF, -1.0, -HALF, 0.0, HALF)
@@ -78,10 +77,11 @@
 
 
 def swath_kernel(
-    cuts, coef, shift, dest, valid, first, last, az_coef, az_base, image,
-    got, notes,
-    held, edge, dense, weight, sent, memo, start, order,
-    ready, own_sem, halo_send, halo_recv, edge_send, edge_recv, send_sem, recv_sem, note_send, note_recv,
+    cuts, coef_in, shift_in, dest_in, valid_in, first_in, last_in, az_coef_in, az_base_in, image,
+    nat, notes,
+    coef, shift, dest, valid, first, last, az_coef, az_base,
+    held, edge, dense, weight, sent, got, memo, start, order,
+    ready, load_sem, own_sem, halo_send, halo_recv, edge_send, edge_recv, send_sem, recv_sem, note_send, note_recv,
 ):
     blocks, cols = image.shape[1], image.shape[2]
     tiles = cols // 128
@@ -89,52 +89,93 @@
     count = lax.axis_size("az")
     me = lax.axis_index("az")
     after, before = lax.rem(me + 1, count), lax.rem(me + count - 1, count)
+    up, down = me < count - 1, me > 0
+
+    barrier = pltpu.get_barrier_semaphore()
+    near = min(NEAR, count - 1)
+
+    def greet(semaphore, step):
+        @pl.when(me + step < count)
+        def _():
+            pl.semaphore_signal(semaphore, inc=1, device_id={"az": lax.rem(me + step, count)})
+
+        @pl.when(me >= step)
+        def _():
+            pl.semaphore_signal(semaphore, inc=1, device_id={"az": lax.rem(me + count - step, count)})
+
+    for step in range(1, near + 1):
+        greet(barrier, step)
     own = pltpu.make_async_copy(image, held.at[:, pl.ds(0, blocks)], own_sem)
     own.start()
-
-    barrier = pltpu.get_barrier_semaphore()
-
-    for peer in (after, before):
-        pl.semaphore_signal(barrier, inc=1, device_id={"az": peer})
+    loads = [
+        pltpu.make_async_copy(source, target, load_sem.at[k])
+        for k, (source, target) in enumerate(
+            (
+                (valid_in, valid), (first_in, first), (last_in, last), (coef_in, coef),
+                (shift_in, shift), (dest_in, dest), (az_coef_in, az_coef), (az_base_in, az_base),
+            )
+        )
+    ]
+    for load in loads:
+        load.start()
+    for load in loads:
+        load.wait()
     low_edge = [jnp.where(valid[r] > 0, first[r], cols) for r in range(blocks)]
     high_edge = [jnp.where(valid[r] > 0, last[r], 0) for r in range(blocks)]
     edge[0, pl.ds(0, blocks), :] = column(low_edge).astype(jnp.float32)
     edge[1, pl.ds(0, blocks), :] = column(high_edge).astype(jnp.float32)
-    pl.semaphore_wait(barrier, 2)
-
-    steps = cols // STEP
+    own.wait()
+    pl.semaphore_wait(barrier, jnp.minimum(me, near) + jnp.minimum(count - 1 - me, near))
+
     chunks = len(cuts) - 1
-    per = steps // (tiles // 16)
-    bounds = [0] + [cut * per + 1 for cut in cuts[1:-1]] + [steps]
-    ways = ((after, blocks - HALO, blocks), (before, 0, blocks + HALO))
-    for w, (peer, source, slot) in enumerate(ways):
-        pltpu.make_async_remote_copy(
-            src_ref=edge.at[:, pl.ds(source, HALO), :],
-            dst_ref=edge.at[:, pl.ds(slot, HALO), :],
-            send_sem=edge_send.at[w],
-            recv_sem=edge_recv.at[w],
-            device_id={"az": peer},
-        ).start()
+    bounds = [0] + [cut * 16 + 1 for cut in cuts[1:-1]] + [tiles]
+    ways = ((after, blocks - HALO, blocks, up, down), (before, 0, blocks + HALO, down, up))
+
+    def begin(copy, sends):
+        @pl.when(sends)
+        def _():
+            copy.start()
+
+    def finish(copy, sends, receives):
+        @pl.when(sends)
+        def _():
+            copy.wait_send()
+
+        @pl.when(receives)
+        def _():
+            copy.wait_recv()
+
     halo = []
     for c in range(chunks):
-        at = pl.ds(bounds[c] * STEP, (bounds[c + 1] - bounds[c]) * STEP)
-        for w, (peer, source, slot) in enumerate(ways):
+        at = pl.ds(bounds[c] * 128, (bounds[c + 1] - bounds[c]) * 128)
+        for w, (peer, source, slot, sends, receives) in enumerate(ways):
             copy = pltpu.make_async_remote_copy(
-                src_ref=image.at[:, pl.ds(source, HALO), at],
+                src_ref=held.at[:, pl.ds(source, HALO), at],
                 dst_ref=held.at[:, pl.ds(slot, HALO), at],
                 send_sem=halo_send.at[c, w],
                 recv_sem=halo_recv.at[c, w],
                 device_id={"az": peer},
             )
-            copy.start()
-            halo.append(copy)
-
-    def meet(r):
-        for peer in (lax.rem(me + (1 << r), count), lax.rem(me + count - (1 << r), count)):
-            pl.semaphore_signal(ready.at[r], inc=1, device_id={"az": peer})
-
-    meetings = ready.shape[0]
-    meet(0)
+            begin(copy, sends)
+            halo.append((copy, sends, receives))
+        if c == 0:
+            bounds_sent = []
+            for w, (peer, source, slot, sends, receives) in enumerate(ways):
+                copy = pltpu.make_async_remote_copy(
+                    src_ref=edge.at[:, pl.ds(source, HALO), :],
+                    dst_ref=edge.at[:, pl.ds(slot, HALO), :],
+                    send_sem=edge_send.at[w],
+                    recv_sem=edge_recv.at[w],
+                    device_id={"az": peer},
+                )
+                begin(copy, sends)
+                bounds_sent.append((copy, sends, receives))
+
+    reach = near
+    stage = 0
+    if reach < count - 1:
+        greet(ready.at[0], reach)
+
     lines = []
     for i in range(blocks):
         target = send_order(me, count, i)
@@ -150,24 +191,17 @@
     fraction = c0 + c1 * q + c2 * q * q
     band = azimuth_band(fraction, column([az_base[j] for j in lines]), column(lines), blocks)
     band = band[:, : blocks + 2 * HALO]
-    pl.semaphore_wait(ready.at[0], 2)
-    if meetings > 1:
-        meet(1)
     range_weights(coef, start, weight, cols)
-    for r in range(1, meetings):
-        pl.semaphore_wait(ready.at[r], 2)
-        if r + 1 < meetings:
-            meet(r + 1)
-
-    own.wait()
-    for w, (peer, source, slot) in enumerate(ways):
-        pltpu.make_async_remote_copy(
-            src_ref=edge.at[:, pl.ds(source, HALO), :],
-            dst_ref=edge.at[:, pl.ds(slot, HALO), :],
-            send_sem=edge_send.at[w],
-            recv_sem=edge_recv.at[w],
-            device_id={"az": peer},
-        ).wait()
+    while reach < count - 1:
+        pl.semaphore_wait(
+            ready.at[stage], (me >= reach).astype(jnp.int32) + (me + reach < count).astype(jnp.int32)
+        )
+        reach, stage = 2 * reach, stage + 1
+        if reach < count - 1:
+            greet(ready.at[stage], reach)
+
+    for copy, sends, receives in bounds_sent:
+        finish(copy, sends, receives)
     low = edge[0]
     high = edge[1]
     row = lax.broadcasted_iota(jnp.int32, high.shape, 0)
@@ -179,11 +213,11 @@
     lane_row = lax.broadcasted_iota(jnp.int32, (blocks, 128), 1)
     lane = lax.broadcasted_iota(jnp.int32, (8, 128), 1)
 
-    def azimuth(s, tails):
-        at = pl.ds(pl.multiple_of(s * STEP, STEP), STEP)
+    def azimuth(first_tile, wide, tails):
+        at = pl.ds(first_tile * 128, wide * 128)
         keeps = []
-        for u in range(STEP // 128):
-            col = lane_held + (s * STEP + u * 128).astype(jnp.float32)
+        for u in range(wide):
+            col = lane_held + ((first_tile + u) * 128.0)
             keeps.append((col >= low) & (col < high))
         new_tails = []
         for p in range(2):
@@ -198,9 +232,9 @@
             out = jnp.dot(band, rows, preferred_element_type=jnp.float32)
             out = out.astype(jnp.bfloat16).astype(jnp.float32)
             tail = tails[p]
-            for u in range(STEP // 128):
+            for u in range(wide):
                 turned = pltpu.roll(out[:, u * 128 : u * 128 + 128], 64, 1)
-                place = p * blocks * span + s * (STEP // 128) + u
+                place = p * blocks * span + first_tile + u
                 dense[pl.ds(place, blocks, stride=span), :] = jnp.where(lane_row < 64, tail, turned)
                 tail = turned
             new_tails.append(tail)
@@ -227,110 +261,141 @@
             power = power + wide * wide
         return power
 
+    def parcel(c, i):
+        at = pl.ds(cuts[c] * 16, (cuts[c + 1] - cuts[c]) * 16)
+        peer = send_order(me, count, i)
+        return pltpu.make_async_remote_copy(
+            src_ref=sent.at[i, :, at, :],
+            dst_ref=got.at[me, :, at, :],
+            send_sem=send_sem.at[c, i],
+            recv_sem=recv_sem.at[c, me],
+            device_id={"az": peer},
+        )
+
     tails = (jnp.zeros((blocks, 128), jnp.float32),) * 2
     power = jnp.zeros((16, 128), jnp.float32)
     for c in range(chunks):
-        for copy in halo[2 * c : 2 * c + 2]:
-            copy.wait()
-        tails = lax.fori_loop(bounds[c], bounds[c + 1], azimuth, tails)
+        for copy, sends, receives in halo[2 * c : 2 * c + 2]:
+            finish(copy, sends, receives)
+        for first_tile in range(bounds[c], bounds[c + 1], WIDE):
+            tails = azimuth(first_tile, min(WIDE, bounds[c + 1] - first_tile), tails)
         if c == chunks - 1:
             for p in range(2):
                 ends = jnp.where(lane_row < 64, tails[p], 0.0)
                 dense[pl.ds(p * blocks * span + tiles, blocks, stride=span), :] = ends
         lo, hi = cuts[c], cuts[c + 1]
-        at = pl.ds(lo * 16, (hi - lo) * 16)
 
         def line(i, power):
             power = lax.fori_loop(lo, hi, functools.partial(filtered, i), power, unroll=True)
-
-            @pl.when(i < count - 1)
-            def _():
-                pltpu.make_async_remote_copy(
-                    src_ref=sent.at[i, :, at, :],
-                    dst_ref=got.at[me, :, at, :],
-                    send_sem=send_sem.at[c, i],
-                    recv_sem=recv_sem.at[c, me],
-                    device_id={"az": send_order(me, count, i)},
-                ).start()
+            if c < chunks - 1:
+
+                @pl.when(i < count - 1)
+                def _():
+                    parcel(c, i).start()
 
             return power
 
         power = lax.fori_loop(0, blocks, line, power)
 
-    own_power = jnp.broadcast_to(jnp.sum(power, keepdims=True), (NOTE, 128))
+    own_power = jnp.broadcast_to(jnp.sum(power, keepdims=True), (1, 128))
     have = jnp.int32(0)
     for j in range(blocks):
         have = have + jnp.maximum(
             jnp.minimum(high_edge[j], cols) - jnp.maximum(low_edge[j], 0), 0
         )
-    own_count = jnp.full((NOTE, 128), have, jnp.int32).astype(jnp.float32)
-    row = lax.broadcasted_iota(jnp.int32, (NOTE, 128), 0)
-    stats = jnp.where(row == 1, own_power, own_count)
+    own_count = jnp.full((1, 128), have, jnp.int32).astype(jnp.float32)
+    lane_note = lax.broadcasted_iota(jnp.int32, (1, 128), 1)
+    stats = jnp.where(lane_note == 127, own_power, own_count)
     for i in range(blocks):
-        place = jnp.full((NOTE, 128), dest[lines[i]] % blocks, jnp.int32).astype(jnp.float32)
-        memo[i] = jnp.where(row == 0, place, stats)
-
-    def tell(i, carry):
-        pltpu.make_async_remote_copy(
+        place = jnp.full((1, 128), dest[lines[i]] % blocks, jnp.int32).astype(jnp.float32)
+        memo[i] = jnp.where(lane_note < 126, place, stats)
+
+    def told(i):
+        return pltpu.make_async_remote_copy(
             src_ref=memo.at[i],
             dst_ref=notes.at[me],
             send_sem=note_send.at[i],
             recv_sem=note_recv.at[me],
             device_id={"az": send_order(me, count, i)},
-        ).start()
+        )
+
+    def tell(i, carry):
+        told(i).start()
         return carry
 
+    def last_send(i, carry):
+        parcel(chunks - 1, i).start()
+        return carry
+
     lax.fori_loop(0, count - 1, tell, 0)
+    lax.fori_loop(0, count - 1, last_send, 0)
     notes[me] = memo[blocks - 1]
     got[me] = sent[blocks - 1]
 
-    def take(i, carry):
-        peer = send_order(me, count, i)
-        for c in range(chunks):
-            lo, hi = cuts[c], cuts[c + 1]
-            at = pl.ds(lo * 16, (hi - lo) * 16)
-            done = pltpu.make_async_remote_copy(
+    for c in range(chunks):
+        lo, wide = cuts[c] * 16, (cuts[c + 1] - cuts[c]) * 16
+        at = pl.ds(lo, wide)
+
+        def take(i, carry):
+            peer = send_order(me, count, i)
+            parcel(c, i).wait_send()
+            pltpu.make_async_remote_copy(
                 src_ref=sent.at[i, :, at, :],
                 dst_ref=got.at[peer, :, at, :],
                 send_sem=send_sem.at[c, i],
                 recv_sem=recv_sem.at[c, peer],
                 device_id={"az": peer},
-            )
-            done.wait_send()
-            done.wait_recv()
-        told = pltpu.make_async_remote_copy(
+            ).wait_recv()
+            return carry
+
+        lax.fori_loop(0, count - 1, take, 0)
+
+        def spread(s, carry):
+            for p in range(2):
+                dense[pl.ds((p * blocks + s) * span + lo, wide), :] = got[s, p, at, :].astype(jnp.float32)
+            return carry
+
+        lax.fori_loop(0, blocks, spread, 0)
+        for t in range(lo, lo + wide):
+            for p in range(2):
+                x = dense[pl.ds(p * blocks * span + t, blocks, stride=span), :]
+                nat[p, :, t * 128 : t * 128 + 128] = x.astype(jnp.bfloat16)
+
+    def hear(i, carry):
+        peer = send_order(me, count, i)
+        told(i).wait_send()
+        pltpu.make_async_remote_copy(
             src_ref=memo.at[i],
             dst_ref=notes.at[peer],
             send_sem=note_send.at[i],
             recv_sem=note_recv.at[peer],
             device_id={"az": peer},
-        )
-        told.wait_send()
-        told.wait_recv()
+        ).wait_recv()
         return carry
 
-    lax.fori_loop(0, count - 1, take, 0)
-
-
-def finish_kernel(total, got, notes, out, mean, share, wide):
+    lax.fori_loop(0, count - 1, hear, 0)
+
+
+def finish_kernel(total, nat, notes, out, mean, share):
     blocks, cols = out.shape[1], out.shape[2]
-    tiles = cols // 128
     told = [notes[s] for s in range(blocks)]
     both = functools.reduce(lambda a, b: a + b, told)
-    power, count = both[1:2], both[2:3]
+    power, count = both[:, 127:128], both[:, 126:127]
     mean_power = power / jnp.maximum(count, 1.0)
     gain = lax.rsqrt(mean_power + 0.5)
+    lane = lax.broadcasted_iota(jnp.int32, (1, 128), 1)
+    place = functools.reduce(
+        lambda a, s: jnp.where(lane == s, told[s], a), range(blocks), jnp.full((1, 128), -1.0)
+    )
+    row = lax.broadcasted_iota(jnp.int32, (blocks, 128), 0).astype(jnp.float32)
+    pick = (row == place).astype(jnp.float32).astype(jnp.bfloat16)[:, :blocks]
+    for p in range(2):
+        for t in range(0, cols, 1024):
+            wide = min(1024, cols - t)
+            x = jnp.dot(pick, nat[p, :, t : t + wide], preferred_element_type=jnp.float32)
+            out[p, :, t : t + wide] = (x * gain).astype(jnp.bfloat16)
     mean[0] = mean_power[0, 0]
     share[0] = (count / float(total))[0, 0]
-    for s in range(blocks):
-        place = told[s][0, 0].astype(jnp.int32)
-        for p in range(2):
-            x = got[s, p].astype(jnp.float32) * gain
-            wide[pl.ds(pl.multiple_of((p * blocks + place) * tiles, 8), tiles), :] = x
-    for t in range(tiles):
-        for p in range(2):
-            x = wide[pl.ds(p * blocks * tiles + t, blocks, stride=tiles), :]
-            out[p, :, t * 128 : t * 128 + 128] = x.astype(jnp.bfloat16)
 
 
 def shards(
@@ -344,28 +409,39 @@
     cuts = [0] + sorted({bigs * cut // 6 for cut in CUTS} - {0, bigs}) + [bigs]
     chunks = len(cuts) - 1
     parts = max(c for c in range(1, PARTS + 1) if bigs % c == 0)
+    vmem = pl.BlockSpec(memory_space=pltpu.VMEM)
     smem = pl.BlockSpec(memory_space=pltpu.SMEM)
-    vmem = pl.BlockSpec(memory_space=pltpu.VMEM)
     held = blocks + 2 * HALO
     dma = pltpu.SemaphoreType.DMA
-    got, notes = pl.pallas_call(
+    stages = max(1, (-(-count // NEAR)).bit_length())
+    nat, notes = pl.pallas_call(
         functools.partial(swath_kernel, cuts),
         out_shape=(
-            jax.ShapeDtypeStruct((blocks, 2, tiles, 128), jnp.bfloat16),
-            jax.ShapeDtypeStruct((blocks, NOTE, 128), jnp.float32),
+            jax.ShapeDtypeStruct((2, blocks, cols), jnp.bfloat16),
+            jax.ShapeDtypeStruct((blocks, 1, 128), jnp.float32),
         ),
-        in_specs=[smem] * 8 + [pl.BlockSpec(memory_space=pl.ANY)],
+        in_specs=[pl.BlockSpec(memory_space=pl.ANY)] * 9,
         out_specs=(vmem, vmem),
         scratch_shapes=[
+            pltpu.SMEM(rg_coef.shape, jnp.float32),
+            pltpu.SMEM((blocks,), jnp.int32),
+            pltpu.SMEM((blocks,), jnp.int32),
+            pltpu.SMEM((blocks,), jnp.int32),
+            pltpu.SMEM((blocks,), jnp.int32),
+            pltpu.SMEM((blocks,), jnp.int32),
+            pltpu.SMEM(az_coef.shape, jnp.float32),
+            pltpu.SMEM((blocks,), jnp.int32),
             pltpu.VMEM((2, held, cols), jnp.bfloat16),
             pltpu.VMEM((2, held, 128), jnp.float32),
             pltpu.VMEM((2 * blocks * (tiles + 8), 128), jnp.float32),
             pltpu.VMEM((tiles // 8, TAPS, 8, 128), jnp.float32),
             pltpu.VMEM((blocks, 2, tiles, 128), jnp.bfloat16),
-            pltpu.VMEM((blocks, NOTE, 128), jnp.float32),
+            pltpu.VMEM((blocks, 2, tiles, 128), jnp.bfloat16),
+            pltpu.VMEM((blocks, 1, 128), jnp.float32),
             pltpu.SMEM((tiles // 8,), jnp.int32),
             pltpu.SMEM((blocks,), jnp.int32),
-            pltpu.SemaphoreType.REGULAR((max(1, (count // 2 - 1).bit_length()),)),
+            pltpu.SemaphoreType.REGULAR((stages,)),
+            dma((8,)),
             dma(()),
             dma((chunks, 2)),
             dma((chunks, 2)),
@@ -390,15 +466,16 @@
             jax.ShapeDtypeStruct((1,), jnp.float32),
         ),
         grid=(parts,),
-        in_specs=[pl.BlockSpec((blocks, 2, tiles // parts, 128), lambda c: (0, 0, c, 0)), vmem],
+        in_specs=[pl.BlockSpec((2, blocks, cols // parts), lambda c: (0, 0, c)), vmem],
         out_specs=(pl.BlockSpec((2, blocks, cols // parts), lambda c: (0, 0, c)), smem, smem),
-        scratch_shapes=[pltpu.VMEM((2 * blocks * (tiles // parts), 128), jnp.float32)],
         name="finish",
-    )(got, notes)
-
-
-CUTS = (2,)
+    )(nat, notes)
+
+
+CUTS = (1, 3)
 PARTS = 2
+NEAR = 4
+WIDE = 9
 
 
 def solution(mesh):

time: 39.6 us -> 35.4 us (0.89)
  Pallas kernels: 38.8 us -> 34.6 us
    pallas_call x1, Pallas kernels: 36.2 us -> 32.3 us  [shards(): pl.pallas_call(functools.partial(swath_kernel, cuts), out_shape=(jax.Shap...]
where the time goes in v1:
time: 35.4 us; the launch traced here: 35.2 us
  Pallas kernels  34.6 us (98%)
  between operations  0.64 us (2%)
    pallas_call x1, Pallas kernels, shards(): pl.pallas_call(functools.partial(swath_kernel, cuts), out_shape=(jax.Shap...  32.3 us
    pallas_call x1, Pallas kernels, shards(): pl.pallas_call(functools.partial(finish_kernel, cols * blocks * count), o...  2.31 us

profile of v1, /device:TPU:0, one launch (start us, length us, event | category | flops | bytes accessed | tf_op | source)
XLA Modules:
  0.0 35.2 jit_solution(1186402099850146839)
XLA Ops:
  0.6 32.3 %swath.1 = (bf16[2,16,12288]{2,1,0:T(8,128)(2,1)}, f32[16,1,128]{2,1,0:T(1,128)}) custom-call(f32[4]{0:T(128)} %coef_in.1, s32[16]{0:T(128)} %shift_in.1, s32[16]{0:T(128)} %dest_in.1, s32[16]{0:T(128)} %valid_in.1, s32[16]{0:T(128)} %first_in.1, s32[16]{0:T(128)} %last_in.1, f32[3,16]{1,0:T(4,128)} %az_coef_in.1, s32[16]{0:T(128)} %az_base_in.1, ...), custom_call_target="tpu_custom_call" | custom-call | tf_op jit(solution)/shard_map/swath/pallas_call | solution.py:417
  32.9 2.3 %finish.1 = (bf16[2,16,12288]{2,1,0:T(8,128)(2,1)}, f32[1]{0:T(128)}, f32[1]{0:T(128)}) custom-call(bf16[2,16,12288]{2,1,0:T(8,128)(2,1)} %get-tuple-element.5.nat, f32[16,1,128]{2,1,0:T(1,128)} %get-tuple-element.6.notes), custom_call_target="tpu_custom_call" | custom-call | tf_op jit(solution)/shard_map/finish/pallas_call | solution.py:461

commit v2 on v1

--- a/solution.py
+++ b/solution.py
@@ -73,7 +73,13 @@
     mine = me // half
     own = i // half
     side = mine * own + (1 - mine) * (1 - own)
-    return side * half + lax.rem(me - mine * half + own + i - own * half, half)
+    near = lax.rem(me - mine * half + own + i - own * half, half)
+    if half % 2:
+        return side * half + near
+    quarter = half // 2
+    group = i // quarter
+    far = (mine * group + (1 - mine) * (1 - group)) * quarter + lax.rem(me + i, quarter)
+    return side * half + jnp.where(own == 1, near, far)
 
 
 def swath_kernel(
@@ -376,7 +382,7 @@
     lax.fori_loop(0, count - 1, hear, 0)
 
 
-def finish_kernel(total, nat, notes, out, mean, share):
+def finish_kernel(total, parts, nat, notes, out, mean, share, scaled, done):
     blocks, cols = out.shape[1], out.shape[2]
     told = [notes[s] for s in range(blocks)]
     both = functools.reduce(lambda a, b: a + b, told)
@@ -389,13 +395,24 @@
     )
     row = lax.broadcasted_iota(jnp.int32, (blocks, 128), 0).astype(jnp.float32)
     pick = (row == place).astype(jnp.float32).astype(jnp.bfloat16)[:, :blocks]
-    for p in range(2):
-        for t in range(0, cols, 1024):
-            wide = min(1024, cols - t)
-            x = jnp.dot(pick, nat[p, :, t : t + wide], preferred_element_type=jnp.float32)
-            out[p, :, t : t + wide] = (x * gain).astype(jnp.bfloat16)
+    copies = []
+    piece = cols // parts
+    for c in range(parts):
+        for p in range(2):
+            for t in range(c * piece, (c + 1) * piece, 1024):
+                wide = min(1024, (c + 1) * piece - t)
+                x = jnp.dot(pick, nat[p, :, t : t + wide], preferred_element_type=jnp.float32)
+                scaled[p, :, t : t + wide] = (x * gain).astype(jnp.bfloat16)
+            at = pl.ds(c * piece, piece)
+            copy = pltpu.make_async_copy(
+                scaled.at[p, :, at], out.at[p, :, at], done.at[2 * c + p]
+            )
+            copy.start()
+            copies.append(copy)
     mean[0] = mean_power[0, 0]
     share[0] = (count / float(total))[0, 0]
+    for copy in copies:
+        copy.wait()
 
 
 def shards(
@@ -417,8 +434,8 @@
     nat, notes = pl.pallas_call(
         functools.partial(swath_kernel, cuts),
         out_shape=(
-            jax.ShapeDtypeStruct((2, blocks, cols), jnp.bfloat16),
-            jax.ShapeDtypeStruct((blocks, 1, 128), jnp.float32),
+            pltpu.VMEM((2, blocks, cols), jnp.bfloat16),
+            pltpu.VMEM((blocks, 1, 128), jnp.float32),
         ),
         in_specs=[pl.BlockSpec(memory_space=pl.ANY)] * 9,
         out_specs=(vmem, vmem),
@@ -459,17 +476,20 @@
         secondary,
     )
     return pl.pallas_call(
-        functools.partial(finish_kernel, cols * blocks * count),
+        functools.partial(finish_kernel, cols * blocks * count, parts),
         out_shape=(
             jax.ShapeDtypeStruct((2, blocks, cols), jnp.bfloat16),
             jax.ShapeDtypeStruct((1,), jnp.float32),
             jax.ShapeDtypeStruct((1,), jnp.float32),
         ),
-        grid=(parts,),
-        in_specs=[pl.BlockSpec((2, blocks, cols // parts), lambda c: (0, 0, c)), vmem],
-        out_specs=(pl.BlockSpec((2, blocks, cols // parts), lambda c: (0, 0, c)), smem, smem),
+        in_specs=[vmem, vmem],
+        out_specs=(pl.BlockSpec(memory_space=pl.ANY), smem, smem),
+        scratch_shapes=[pltpu.VMEM((2, blocks, cols), jnp.bfloat16), dma((2 * parts,))],
         name="finish",
-    )(nat, notes)
+    )(
+        pltpu.with_memory_space_constraint(nat, pltpu.VMEM),
+        pltpu.with_memory_space_constraint(notes, pltpu.VMEM),
+    )
 
 
 CUTS = (1, 3)

time: 35.4 us -> 32.4 us (0.915)
  Pallas kernels: 34.6 us -> 31.6 us
    pallas_call x2, Pallas kernels: 34.6 us -> 31.6 us  [the longest x1 29.9 us: shards(): pl.pallas_call(functools.partial(swath_kernel, cuts), out_shape=(pltpu.VM...]
where the time goes in v2:
time: 32.4 us; the launch traced here: 32.2 us
  Pallas kernels  31.6 us (98%)
  between operations  0.64 us (2%)
    pallas_call x1, Pallas kernels, shards(): pl.pallas_call(functools.partial(swath_kernel, cuts), out_shape=(pltpu.VM...  29.9 us
    pallas_call x1, Pallas kernels, shards(): pl.pallas_call(functools.partial(finish_kernel, cols * blocks * count, pa...  1.65 us

profile of v2, /device:TPU:0, one launch (start us, length us, event | category | flops | bytes accessed | tf_op | source)
XLA Modules:
  0.0 32.2 jit_solution(10429084902637452468)
XLA Ops:
  0.6 29.9 %swath.1 = (bf16[2,16,12288]{2,1,0:T(8,128)(2,1)S(1)}, f32[16,1,128]{2,1,0:T(1,128)S(1)}) custom-call(f32[4]{0:T(128)} %coef_in.1, s32[16]{0:T(128)} %shift_in.1, s32[16]{0:T(128)} %dest_in.1, s32[16]{0:T(128)} %valid_in.1, s32[16]{0:T(128)} %first_in.1, s32[16]{0:T(128)} %last_in.1, f32[3,16]{1,0:T(4,128)} %az_coef_in.1, s32[16]{0:T(128)} %az_base_in.1, ...), custom_call_target="tpu_custom_call" | custom-call | tf_op jit(solution)/shard_map/swath/pallas_call | solution.py:434
  30.6 1.6 %finish.1 = (bf16[2,16,12288]{2,1,0:T(8,128)(2,1)}, f32[1]{0:T(128)}, f32[1]{0:T(128)}) custom-call(bf16[2,16,12288]{2,1,0:T(8,128)(2,1)S(1)} %get-tuple-element.5.nat, f32[16,1,128]{2,1,0:T(1,128)S(1)} %get-tuple-element.6.notes), custom_call_target="tpu_custom_call" | custom-call | tf_op jit(solution)/shard_map/finish/pallas_call | solution.py:478

commit v3 on v2

--- a/solution.py
+++ b/solution.py
@@ -1,4 +1,5 @@
 import functools
+import math
 
 import jax
 import jax.numpy as jnp
@@ -8,22 +9,33 @@
 from jax.sharding import PartitionSpec as P
 
 HALO = 8
-TAPS = 11
+GROUP = 2048
+RANGE_LIMIT = 3.0
 NOTE = 8
 PI = 3.141592653589793
 HALF = 0.7071067811865476
 COS8 = (1.0, HALF, 0.0, -HALF, -1.0, -HALF, 0.0, HALF)
 
 
+def range_spread(cols):
+    half = GROUP / 2 / cols
+    return RANGE_LIMIT * (half + 1.0 - (1.0 - half) ** 2 + 1.0 - (1.0 - half) ** 3) + 0.03
+
+
+def range_taps(cols):
+    return math.ceil(2.0 * (4.0 + range_spread(cols)))
+
+
 def range_weights(coef, start, weight, cols):
-    for g in range(cols // 1024):
-        centre = (g * 1024 + 512) / cols
+    reach = 4.0 + range_spread(cols)
+    for g in range(cols // GROUP):
+        centre = (g + 0.5) * GROUP / cols
         oc = coef[0] + coef[1] * centre + coef[2] * (centre * centre) + coef[3] * (centre**3)
-        n0 = (oc - 5.0 + 64.0).astype(jnp.int32) - 63
+        n0 = (oc - reach + 64.0).astype(jnp.int32) - 63
         start[g] = n0
-        sub = lax.broadcasted_iota(jnp.int32, (8, 128), 0)
-        lane = lax.broadcasted_iota(jnp.int32, (8, 128), 1)
-        col = g * 1024 + sub * 128 + lane
+        sub = lax.broadcasted_iota(jnp.int32, (GROUP // 128, 128), 0)
+        lane = lax.broadcasted_iota(jnp.int32, (GROUP // 128, 128), 1)
+        col = g * GROUP + sub * 128 + lane
         v = (col.astype(jnp.float32) + 0.5) / cols
         off = coef[0] + coef[1] * v + coef[2] * v * v + coef[3] * v * v * v
         whole = jnp.round(off)
@@ -32,7 +44,7 @@
         sine = jnp.sin(PI * part) * (-1.0 / PI) * (1 - 2 * odd).astype(jnp.float32)
         base = (n0.astype(jnp.float32) - off) * (PI / 4.0)
         c0, s0 = jnp.cos(base), jnp.sin(base)
-        for k in range(TAPS):
+        for k in range(weight.shape[1]):
             n = n0 + k
             d = n.astype(jnp.float32) - off
             ck, sk = COS8[k % 8], COS8[(k - 2) % 8]
@@ -217,7 +229,7 @@
     high = jnp.where(outside, 0.0, high)
     lane_held = lax.broadcasted_iota(jnp.int32, high.shape, 1).astype(jnp.float32)
     lane_row = lax.broadcasted_iota(jnp.int32, (blocks, 128), 1)
-    lane = lax.broadcasted_iota(jnp.int32, (8, 128), 1)
+    lane = lax.broadcasted_iota(jnp.int32, (16, 128), 1)
 
     def azimuth(first_tile, wide, tails):
         at = pl.ds(first_tile * 128, wide * 128)
@@ -247,21 +259,17 @@
         return tuple(new_tails)
 
     def filtered(i, big, power):
+        b = shift[order[i]] + start[big] + 64
         for p in range(2):
-            halves = []
-            for h in range(2):
-                g = big * 2 + h
-                b = shift[order[i]] + start[g] + 64
-                at = pl.multiple_of((p * blocks + i) * span + g * 8, 8)
-                x0 = dense[pl.ds(at, 8), :]
-                x1 = dense[pl.ds(at + 1, 8), :]
-                acc = None
-                for k in range(TAPS):
-                    moved = pltpu.roll(jnp.where(lane < b + k, x1, x0), 128 - b - k, 1)
-                    term = weight[g, k] * moved
-                    acc = term if acc is None else acc + term
-                halves.append(acc)
-            done = jnp.concatenate(halves, axis=0).astype(jnp.bfloat16)
+            at = pl.multiple_of((p * blocks + i) * span + big * 16, 8)
+            x0 = dense[pl.ds(at, 16), :]
+            x1 = dense[pl.ds(at + 1, 16), :]
+            acc = None
+            for k in range(weight.shape[1]):
+                moved = pltpu.roll(jnp.where(lane < b + k, x1, x0).astype(jnp.bfloat16), 128 - b - k, 1)
+                term = weight[big, k] * moved.astype(jnp.float32)
+                acc = term if acc is None else acc + term
+            done = acc.astype(jnp.bfloat16)
             sent[i, p, pl.ds(pl.multiple_of(big * 16, 16), 16), :] = done
             wide = done.astype(jnp.float32)
             power = power + wide * wide
@@ -280,6 +288,31 @@
 
     tails = (jnp.zeros((blocks, 128), jnp.float32),) * 2
     power = jnp.zeros((16, 128), jnp.float32)
+    half = count // 2
+    far, near_half, own_half = (0, half // 2), (half // 2, half), (half, blocks)
+
+    def post(c, lines_at):
+        def body(i, carry):
+            parcel(c, i).start()
+            return carry
+
+        lax.fori_loop(lines_at[0], min(lines_at[1], count - 1), body, 0)
+
+    def lines_of(c, lines_at, power, send):
+        def line(i, power):
+            power = lax.fori_loop(
+                cuts[c], cuts[c + 1], functools.partial(filtered, i), power, unroll=True
+            )
+            if send:
+
+                @pl.when(i < count - 1)
+                def _():
+                    parcel(c, i).start()
+
+            return power
+
+        return lax.fori_loop(*lines_at, line, power)
+
     for c in range(chunks):
         for copy, sends, receives in halo[2 * c : 2 * c + 2]:
             finish(copy, sends, receives)
@@ -289,19 +322,15 @@
             for p in range(2):
                 ends = jnp.where(lane_row < 64, tails[p], 0.0)
                 dense[pl.ds(p * blocks * span + tiles, blocks, stride=span), :] = ends
-        lo, hi = cuts[c], cuts[c + 1]
-
-        def line(i, power):
-            power = lax.fori_loop(lo, hi, functools.partial(filtered, i), power, unroll=True)
-            if c < chunks - 1:
-
-                @pl.when(i < count - 1)
-                def _():
-                    parcel(c, i).start()
-
-            return power
-
-        power = lax.fori_loop(0, blocks, line, power)
+        power = lines_of(c, far, power, True)
+        if c < chunks - 1:
+            power = lines_of(*((0, near_half) if c == 0 else (c - 1, own_half)), power, True)
+    for c in range(1, chunks - 1):
+        power = lines_of(c, near_half, power, True)
+    power = lines_of(chunks - 1, near_half, power, False)
+    late = [c for c in (chunks - 2, chunks - 1) if c >= 0]
+    for c in late:
+        power = lines_of(c, own_half, power, False)
 
     own_power = jnp.broadcast_to(jnp.sum(power, keepdims=True), (1, 128))
     have = jnp.int32(0)
@@ -329,12 +358,10 @@
         told(i).start()
         return carry
 
-    def last_send(i, carry):
-        parcel(chunks - 1, i).start()
-        return carry
-
     lax.fori_loop(0, count - 1, tell, 0)
-    lax.fori_loop(0, count - 1, last_send, 0)
+    post(chunks - 1, near_half)
+    for c in late:
+        post(c, own_half)
     notes[me] = memo[blocks - 1]
     got[me] = sent[blocks - 1]
 
@@ -382,7 +409,7 @@
     lax.fori_loop(0, count - 1, hear, 0)
 
 
-def finish_kernel(total, parts, nat, notes, out, mean, share, scaled, done):
+def finish_kernel(total, parts, nat, notes, out, mean, share, scaled, figures, done):
     blocks, cols = out.shape[1], out.shape[2]
     told = [notes[s] for s in range(blocks)]
     both = functools.reduce(lambda a, b: a + b, told)
@@ -395,7 +422,13 @@
     )
     row = lax.broadcasted_iota(jnp.int32, (blocks, 128), 0).astype(jnp.float32)
     pick = (row == place).astype(jnp.float32).astype(jnp.bfloat16)[:, :blocks]
-    copies = []
+    figures[0, 0] = mean_power[0, 0]
+    figures[1, 0] = (count / float(total))[0, 0]
+    copies = [
+        pltpu.make_async_copy(figures.at[k], target, done.at[k]) for k, target in enumerate((mean, share))
+    ]
+    for copy in copies:
+        copy.start()
     piece = cols // parts
     for c in range(parts):
         for p in range(2):
@@ -405,12 +438,10 @@
                 scaled[p, :, t : t + wide] = (x * gain).astype(jnp.bfloat16)
             at = pl.ds(c * piece, piece)
             copy = pltpu.make_async_copy(
-                scaled.at[p, :, at], out.at[p, :, at], done.at[2 * c + p]
+                scaled.at[p, :, at], out.at[p, :, at], done.at[2 + 2 * c + p]
             )
             copy.start()
             copies.append(copy)
-    mean[0] = mean_power[0, 0]
-    share[0] = (count / float(total))[0, 0]
     for copy in copies:
         copy.wait()
 
@@ -427,7 +458,6 @@
     chunks = len(cuts) - 1
     parts = max(c for c in range(1, PARTS + 1) if bigs % c == 0)
     vmem = pl.BlockSpec(memory_space=pltpu.VMEM)
-    smem = pl.BlockSpec(memory_space=pltpu.SMEM)
     held = blocks + 2 * HALO
     dma = pltpu.SemaphoreType.DMA
     stages = max(1, (-(-count // NEAR)).bit_length())
@@ -451,11 +481,11 @@
             pltpu.VMEM((2, held, cols), jnp.bfloat16),
             pltpu.VMEM((2, held, 128), jnp.float32),
             pltpu.VMEM((2 * blocks * (tiles + 8), 128), jnp.float32),
-            pltpu.VMEM((tiles // 8, TAPS, 8, 128), jnp.float32),
+            pltpu.VMEM((cols // GROUP, range_taps(cols), GROUP // 128, 128), jnp.float32),
             pltpu.VMEM((blocks, 2, tiles, 128), jnp.bfloat16),
             pltpu.VMEM((blocks, 2, tiles, 128), jnp.bfloat16),
             pltpu.VMEM((blocks, 1, 128), jnp.float32),
-            pltpu.SMEM((tiles // 8,), jnp.int32),
+            pltpu.SMEM((cols // GROUP,), jnp.int32),
             pltpu.SMEM((blocks,), jnp.int32),
             pltpu.SemaphoreType.REGULAR((stages,)),
             dma((8,)),
@@ -483,8 +513,12 @@
             jax.ShapeDtypeStruct((1,), jnp.float32),
         ),
         in_specs=[vmem, vmem],
-        out_specs=(pl.BlockSpec(memory_space=pl.ANY), smem, smem),
-        scratch_shapes=[pltpu.VMEM((2, blocks, cols), jnp.bfloat16), dma((2 * parts,))],
+        out_specs=(pl.BlockSpec(memory_space=pl.ANY),) * 3,
+        scratch_shapes=[
+            pltpu.VMEM((2, blocks, cols), jnp.bfloat16),
+            pltpu.SMEM((2, 1), jnp.float32),
+            dma((2 + 2 * parts,)),
+        ],
         name="finish",
     )(
         pltpu.with_memory_space_constraint(nat, pltpu.VMEM),

time: 32.4 us -> 31.1 us (0.960)
  Pallas kernels: 31.6 us -> 30.2 us
    pallas_call x1, Pallas kernels: 29.9 us -> 29.1 us  [shards(): pl.pallas_call(functools.partial(swath_kernel, cuts), out_shape=(pltpu.VM...]
    pallas_call x1, Pallas kernels: 1.65 us -> 1.15 us  [shards(): pl.pallas_call(functools.partial(finish_kernel, cols * blocks * count, pa...]
where the time goes in v3:
time: 31.1 us; the launch traced here: 30.8 us
  Pallas kernels  30.2 us (97%)
  between operations  0.64 us (2%)
    pallas_call x1, Pallas kernels, shards(): pl.pallas_call(functools.partial(swath_kernel, cuts), out_shape=(pltpu.VM...  29.1 us
    pallas_call x1, Pallas kernels, shards(): pl.pallas_call(functools.partial(finish_kernel, cols * blocks * count, pa...  1.15 us

profile of v3, /device:TPU:0, one launch (start us, length us, event | category | flops | bytes accessed | tf_op | source)
XLA Modules:
  0.0 30.8 jit_solution(3863376388114397770)
XLA Ops:
  0.6 29.1 %swath.1 = (bf16[2,16,12288]{2,1,0:T(8,128)(2,1)S(1)}, f32[16,1,128]{2,1,0:T(1,128)S(1)}) custom-call(f32[4]{0:T(128)} %coef_in.1, s32[16]{0:T(128)} %shift_in.1, s32[16]{0:T(128)} %dest_in.1, s32[16]{0:T(128)} %valid_in.1, s32[16]{0:T(128)} %first_in.1, s32[16]{0:T(128)} %last_in.1, f32[3,16]{1,0:T(4,128)} %az_coef_in.1, s32[16]{0:T(128)} %az_base_in.1, ...), custom_call_target="tpu_custom_call" | custom-call | tf_op jit(solution)/shard_map/swath/pallas_call | solution.py:464
  29.7 1.2 %finish.1 = (bf16[2,16,12288]{2,1,0:T(8,128)(2,1)}, f32[1]{0:T(128)}, f32[1]{0:T(128)}) custom-call(bf16[2,16,12288]{2,1,0:T(8,128)(2,1)S(1)} %get-tuple-element.5.nat, f32[16,1,128]{2,1,0:T(1,128)S(1)} %get-tuple-element.6.notes), custom_call_target="tpu_custom_call" | custom-call | tf_op jit(solution)/shard_map/finish/pallas_call | solution.py:508

commit v4 on v3

--- a/solution.py
+++ b/solution.py
@@ -299,19 +299,24 @@
         lax.fori_loop(lines_at[0], min(lines_at[1], count - 1), body, 0)
 
     def lines_of(c, lines_at, power, send):
-        def line(i, power):
-            power = lax.fori_loop(
-                cuts[c], cuts[c + 1], functools.partial(filtered, i), power, unroll=True
-            )
+        low, high = lines_at
+        step = math.gcd(high - low, TOGETHER)
+
+        def group(g, power):
+            held_lines = [low + g * step + u for u in range(step)]
+            for big in range(cuts[c], cuts[c + 1]):
+                for i in held_lines:
+                    power = filtered(i, big, power)
             if send:
-
-                @pl.when(i < count - 1)
-                def _():
-                    parcel(c, i).start()
+                for i in held_lines:
+
+                    @pl.when(i < count - 1)
+                    def _(i=i):
+                        parcel(c, i).start()
 
             return power
 
-        return lax.fori_loop(*lines_at, line, power)
+        return lax.fori_loop(0, (high - low) // step, group, power)
 
     for c in range(chunks):
         for copy, sends, receives in halo[2 * c : 2 * c + 2]:
@@ -324,13 +329,11 @@
                 dense[pl.ds(p * blocks * span + tiles, blocks, stride=span), :] = ends
         power = lines_of(c, far, power, True)
         if c < chunks - 1:
-            power = lines_of(*((0, near_half) if c == 0 else (c - 1, own_half)), power, True)
-    for c in range(1, chunks - 1):
-        power = lines_of(c, near_half, power, True)
-    power = lines_of(chunks - 1, near_half, power, False)
-    late = [c for c in (chunks - 2, chunks - 1) if c >= 0]
-    for c in late:
-        power = lines_of(c, own_half, power, False)
+            power = lines_of(c, own_half, power, True)
+            power = lines_of(c, near_half, power, True)
+    c = chunks - 1
+    power = lines_of(c, near_half, power, False)
+    power = lines_of(c, own_half, power, False)
 
     own_power = jnp.broadcast_to(jnp.sum(power, keepdims=True), (1, 128))
     have = jnp.int32(0)
@@ -359,9 +362,8 @@
         return carry
 
     lax.fori_loop(0, count - 1, tell, 0)
+    post(chunks - 1, own_half)
     post(chunks - 1, near_half)
-    for c in late:
-        post(c, own_half)
     notes[me] = memo[blocks - 1]
     got[me] = sent[blocks - 1]
 
@@ -528,6 +530,7 @@
 
 CUTS = (1, 3)
 PARTS = 2
+TOGETHER = 4
 NEAR = 4
 WIDE = 9
 

time: 31.1 us -> 30.8 us (level)
  no operation moved by 1% of the time
where the time goes in v4:
time: 30.8 us; the launch traced here: 30.7 us
  Pallas kernels  30 us (97%)
  between operations  0.64 us (2%)
    pallas_call x1, Pallas kernels, shards(): pl.pallas_call(functools.partial(swath_kernel, cuts), out_shape=(pltpu.VM...  28.9 us
    pallas_call x1, Pallas kernels, shards(): pl.pallas_call(functools.partial(finish_kernel, cols * blocks * count, pa...  1.15 us

profile of v4, /device:TPU:0, one launch (start us, length us, event | category | flops | bytes accessed | tf_op | source)
XLA Modules:
  0.0 30.7 jit_solution(1131039970367571895)
XLA Ops:
  0.6 28.9 %swath.1 = (bf16[2,16,12288]{2,1,0:T(8,128)(2,1)S(1)}, f32[16,1,128]{2,1,0:T(1,128)S(1)}) custom-call(f32[4]{0:T(128)} %coef_in.1, s32[16]{0:T(128)} %shift_in.1, s32[16]{0:T(128)} %dest_in.1, s32[16]{0:T(128)} %valid_in.1, s32[16]{0:T(128)} %first_in.1, s32[16]{0:T(128)} %last_in.1, f32[3,16]{1,0:T(4,128)} %az_coef_in.1, s32[16]{0:T(128)} %az_base_in.1, ...), custom_call_target="tpu_custom_call" | custom-call | tf_op jit(solution)/shard_map/swath/pallas_call | solution.py:466
  29.5 1.2 %finish.1 = (bf16[2,16,12288]{2,1,0:T(8,128)(2,1)}, f32[1]{0:T(128)}, f32[1]{0:T(128)}) custom-call(bf16[2,16,12288]{2,1,0:T(8,128)(2,1)S(1)} %get-tuple-element.5.nat, f32[16,1,128]{2,1,0:T(1,128)S(1)} %get-tuple-element.6.notes), custom_call_target="tpu_custom_call" | custom-call | tf_op jit(solution)/shard_map/finish/pallas_call | solution.py:510

commit v5 on v4

--- a/solution.py
+++ b/solution.py
@@ -83,14 +83,17 @@
 def send_order(me, count, i):
     half = count // 2
     mine = me // half
-    own = i // half
+    local = me - mine * half
+    slot = jnp.where(mine == 1, i, lax.rem(i + half, count - 1))
+    slot = jnp.where(i == count - 1, i, slot)
+    own = slot // half
     side = mine * own + (1 - mine) * (1 - own)
-    near = lax.rem(me - mine * half + own + i - own * half, half)
+    near = lax.rem(local + own + slot - own * half, half)
     if half % 2:
         return side * half + near
     quarter = half // 2
-    group = i // quarter
-    far = (mine * group + (1 - mine) * (1 - group)) * quarter + lax.rem(me + i, quarter)
+    group = slot // quarter
+    far = (mine * group + (1 - mine) * (1 - group)) * quarter + lax.rem(me + slot, quarter)
     return side * half + jnp.where(own == 1, near, far)
 
 
@@ -381,16 +384,16 @@
                 recv_sem=recv_sem.at[c, peer],
                 device_id={"az": peer},
             ).wait_recv()
-            return carry
-
-        lax.fori_loop(0, count - 1, take, 0)
+            return spread(peer, carry)
 
         def spread(s, carry):
             for p in range(2):
-                dense[pl.ds((p * blocks + s) * span + lo, wide), :] = got[s, p, at, :].astype(jnp.float32)
+                row = pl.multiple_of((p * blocks + s) * span + lo, 8)
+                dense[pl.ds(row, wide), :] = got[s, p, at, :].astype(jnp.float32)
             return carry
 
-        lax.fori_loop(0, blocks, spread, 0)
+        spread(me, 0)
+        lax.fori_loop(0, count - 1, take, 0)
         for t in range(lo, lo + wide):
             for p in range(2):
                 x = dense[pl.ds(p * blocks * span + t, blocks, stride=span), :]

time: 30.8 us -> 30.8 us (level)
  no operation moved by 1% of the time
where the time goes in v5:
time: 30.8 us; the launch traced here: 30.6 us
  Pallas kernels  30 us (97%)
  between operations  0.64 us (2%)
    pallas_call x1, Pallas kernels, shards(): pl.pallas_call(functools.partial(swath_kernel, cuts), out_shape=(pltpu.VM...  28.8 us
    pallas_call x1, Pallas kernels, shards(): pl.pallas_call(functools.partial(finish_kernel, cols * blocks * count, pa...  1.15 us

profile of v5, /device:TPU:0, one launch (start us, length us, event | category | flops | bytes accessed | tf_op | source)
XLA Modules:
  0.0 30.6 jit_solution(5889527374246786155)
XLA Ops:
  0.6 28.8 %swath.1 = (bf16[2,16,12288]{2,1,0:T(8,128)(2,1)S(1)}, f32[16,1,128]{2,1,0:T(1,128)S(1)}) custom-call(f32[4]{0:T(128)} %coef_in.1, s32[16]{0:T(128)} %shift_in.1, s32[16]{0:T(128)} %dest_in.1, s32[16]{0:T(128)} %valid_in.1, s32[16]{0:T(128)} %first_in.1, s32[16]{0:T(128)} %last_in.1, f32[3,16]{1,0:T(4,128)} %az_coef_in.1, s32[16]{0:T(128)} %az_base_in.1, ...), custom_call_target="tpu_custom_call" | custom-call | tf_op jit(solution)/shard_map/swath/pallas_call | solution.py:469
  29.5 1.2 %finish.1 = (bf16[2,16,12288]{2,1,0:T(8,128)(2,1)}, f32[1]{0:T(128)}, f32[1]{0:T(128)}) custom-call(bf16[2,16,12288]{2,1,0:T(8,128)(2,1)S(1)} %get-tuple-element.5.nat, f32[16,1,128]{2,1,0:T(1,128)S(1)} %get-tuple-element.6.notes), custom_call_target="tpu_custom_call" | custom-call | tf_op jit(solution)/shard_map/finish/pallas_call | solution.py:513
